TPU v7x, 32 devices: a whole 2x2x4 slice. The times are simulated.
32 devices in a mesh: ba: 8 (over y, x, core), wa: 4 (over z).
Axes of the slice: x: 2, y: 2, z: 4, core: 2. Of those that a mesh axis runs over, the one named last changes fastest.
Arguments:
- sky_model: float32 [2, 2048, 2048], P(None, None, 'wa'), may hold values from -6 to 6
- plane_w: float32 [8], P('ba'), may hold values from -60 to 60
- kernel: float32 [16, 8], replicated, may hold values from -2 to 2
- tile_ids: int32 [512], P(('ba', 'wa')), may hold values from 0 to 255, as said below
- plane_ids: int32 [512, 1], P(('ba', 'wa')), may hold values from 0 to 7; in each aligned block of 16 rows (0 to 15, 16 to 31, ...) at most 2 rows name the same one
- positions: int32 [512, 2, 512], P(('ba', 'wa')), may hold values from 0 to 1935
- observed: float32 [512, 2, 512], P(('ba', 'wa')), may hold values from -6 to 6
Outputs:
- residual_vis: float32 [512, 2, 512], P(('ba', 'wa'))
Inputs may be any that keep to these rules, and one draw needn't show every extreme that they name: `plane_ids`: among the 16 blocks of one device at most 2 name the same w-plane, and in every draw some device has a w-plane named by exactly 2 of its blocks. `tile_ids`: A tile id is row_tile * 16 + column_tile; the blocks held at index a of wa name column tiles a * 4 to (a + 1) * 4 - 1.
All inputs are finite; a program needn't handle non-finite values.
Results may differ from a plain program's by a relative error of at most 0.0003.
Values sent between devices are 32-bit elements; how exact they have to be, the bound alone decides.
A program may use at most 128 MiB of HBM per device.

v0:
```python
import math
import jax
import jax.numpy as jnp
from jax import lax
from jax.sharding import PartitionSpec as P

TILE = 128
PRECISE = lax.Precision.HIGHEST
FIELD_WIDTH = 0.7


def product(pattern, operand_a, operand_b):
    return jnp.einsum(pattern, operand_a, operand_b, precision=PRECISE)


def complex_product(pattern, table_pair, values):
    return (
        product(pattern, table_pair[0], values[0]) - product(pattern, table_pair[1], values[1]),
        product(pattern, table_pair[0], values[1]) + product(pattern, table_pair[1], values[0]),
    )


def phase_table(rows_count, cols_count, modulus):
    first_index = jnp.arange(rows_count, dtype=jnp.int32)[:, None]
    second_index = jnp.arange(cols_count, dtype=jnp.int32)[None, :]
    angle_rad = (first_index * second_index % modulus).astype(jnp.float32) * (
        -2.0 * math.pi / modulus
    )
    return (jnp.cos(angle_rad), jnp.sin(angle_rad))


def transform(values, pattern):
    length = values[0].shape[0]
    columns = values[0].shape[1]
    long_side = min(length, 128)
    short_side = length // long_side
    shaped = (
        values[0].reshape(long_side, short_side, columns),
        values[1].reshape(long_side, short_side, columns),
    )
    section_one = complex_product(
        "ab,anl->bnl", phase_table(long_side, long_side, long_side), shaped
    )
    twiddle = phase_table(long_side, short_side, length)
    twist_real = twiddle[0][:, :, None]
    twist_imag = twiddle[1][:, :, None]
    turned = (
        section_one[0] * twist_real - section_one[1] * twist_imag,
        section_one[0] * twist_imag + section_one[1] * twist_real,
    )
    return complex_product(
        "nk,bnl->" + pattern, phase_table(short_side, short_side, short_side), turned
    )


def kernel_rows(fine_position, kernel, tile_side):
    oversample, support = kernel.shape
    cell_index = fine_position // oversample
    offset_index = fine_position % oversample
    picker = (offset_index[..., None] == jnp.arange(oversample, dtype=jnp.int32)).astype(
        jnp.float32
    )
    kernel_taps = product("gso,ok->gsk", picker, kernel)
    tile_cells = jnp.arange(tile_side, dtype=jnp.int32)
    weights = jnp.zeros(fine_position.shape + (tile_side,), jnp.float32)
    for tap_step in range(support):
        weights = weights + jnp.where(
            tile_cells == cell_index[..., None] + tap_step,
            kernel_taps[..., tap_step : tap_step + 1],
            0.0,
        )
    return weights


def degrid(tiles, fine_position, kernel):
    tile_side = tiles.shape[-1]
    row_weights = kernel_rows(fine_position[:, 0], kernel, tile_side)
    col_weights = kernel_rows(fine_position[:, 1], kernel, tile_side)
    partial_value = product("gsu,gcuv->gcsv", row_weights, tiles)
    return jnp.sum(partial_value * col_weights[:, None], axis=-1)


def grouped(function, count, operands):
    group_size = math.gcd(count, 8)
    reshaped = tuple(
        (
            operand.reshape((count // group_size, group_size) + operand.shape[1:])
            for operand in operands
        )
    )

    def apply_group(group_items):
        return function(*group_items)

    result = lax.map(apply_group, reshaped)
    return result.reshape((count,) + result.shape[2:])


def shards(sky_model, plane_w, kernel, tile_ids, plane_ids, positions, observed):
    extent = sky_model.shape[1]
    column_count = sky_model.shape[2]
    slab_index = lax.axis_index("wa")
    spacing = FIELD_WIDTH / extent
    column_coord = (
        (slab_index * column_count + jnp.arange(column_count, dtype=jnp.int32)).astype(jnp.float32)
        - extent / 2
    ) * spacing
    row_coord = (jnp.arange(extent, dtype=jnp.int32).astype(jnp.float32) - extent / 2) * spacing
    radius_sq = row_coord[:, None] ** 2 + column_coord[None, :] ** 2
    lowered = -radius_sq / (1.0 + jnp.sqrt(1.0 - radius_sq))
    phase_angle = -2.0 * math.pi * plane_w[0] * lowered
    cosine = jnp.cos(phase_angle)
    sine_part = jnp.sin(phase_angle)
    image_real = sky_model[0] * cosine - sky_model[1] * sine_part
    image_imag = sky_model[0] * sine_part + sky_model[1] * cosine
    half_done = transform((image_real, image_imag), "lkb")
    stacked = jnp.stack(
        [half_done[0].reshape(column_count, extent), half_done[1].reshape(column_count, extent)]
    )
    exchanged = lax.all_to_all(stacked, "wa", split_axis=2, concat_axis=1, tiled=True)
    finished = transform((exchanged[0], exchanged[1]), "kbl")
    norm_factor = 1.0 / extent
    uv_grid = jnp.stack(
        [
            finished[0].reshape(extent, column_count) * norm_factor,
            finished[1].reshape(extent, column_count) * norm_factor,
        ]
    )
    plane_count = lax.axis_size("ba")
    block_count = tile_ids.shape[0]
    sample_count = positions.shape[2]
    capacity = max(2, block_count // plane_count)
    target = plane_ids[:, 0]
    onehot = (target[:, None] == jnp.arange(plane_count, dtype=jnp.int32)[None, :]).astype(
        jnp.int32
    )
    earlier = jnp.cumsum(onehot, axis=0) - onehot
    rank_in = jnp.sum(earlier * onehot, axis=1)
    slot_index = target * capacity + rank_in
    slot_tiles = jnp.zeros((plane_count * capacity,), jnp.int32).at[slot_index].set(tile_ids)
    slot_tiles = slot_tiles.reshape(plane_count, capacity)
    tile_side = TILE
    tiles_across = extent // tile_side
    local_across = column_count // tile_side

    def cut_tile(tile_number):
        row_tile = tile_number // tiles_across
        col_tile = tile_number % tiles_across - slab_index * local_across
        return lax.dynamic_slice(
            uv_grid,
            (jnp.int32(0), row_tile * tile_side, col_tile * tile_side),
            (2, tile_side, tile_side),
        )

    slot_fine = (
        jnp.zeros((plane_count * capacity, 2, sample_count), jnp.int32)
        .at[slot_index]
        .set(positions)
    )
    slot_fine = slot_fine.reshape(plane_count, capacity, 2, sample_count)
    asked_tiles = lax.all_to_all(slot_tiles, "ba", split_axis=0, concat_axis=0, tiled=True)
    asked_fine = lax.all_to_all(slot_fine, "ba", split_axis=0, concat_axis=0, tiled=True)
    count = asked_tiles.shape[0] * asked_tiles.shape[1]

    def slot_group(tile_group, fine_group):
        return degrid(jax.vmap(cut_tile)(tile_group), fine_group, kernel)

    values = grouped(
        slot_group, count, (asked_tiles.reshape(count), asked_fine.reshape(count, 2, sample_count))
    )
    values = values.reshape(asked_tiles.shape[0], asked_tiles.shape[1], 2, sample_count)
    answers = lax.all_to_all(values, "ba", split_axis=0, concat_axis=0, tiled=True)
    predicted = answers.reshape(plane_count * capacity, 2, sample_count)[slot_index]
    return observed - predicted


def solution(mesh):
    return jax.shard_map(
        shards,
        mesh=mesh,
        in_specs=(
            P(None, None, "wa"),
            P("ba"),
            P(),
            P(("ba", "wa")),
            P(("ba", "wa"), None),
            P(("ba", "wa"), None, None),
            P(("ba", "wa"), None, None),
        ),
        out_specs=P(("ba", "wa"), None, None),
        check_vma=False,
    )
```

profile of v0, /device:TPU:0, one launch (start us, length us, event | category | flops | bytes accessed | tf_op | source)
XLA Modules:
  0.0 576.1 jit_solution(2095315293875353910)
XLA Ops:
  3.7 5.2 all-to-all-start
  9.0 7.7 %fusion.226 = (f32[1,2048,512]{2,1,0:T(8,128)}, f32[1,2048,512]{2,1,0:T(8,128)}) fusion(f32[2,2048,512]{2,1,0:T(8,128)} %param.9), kind=kLoop, calls=%fused_computation.309 | loop fusion | bytes 16777216 | tf_op jit(solution)/shard_map/slice | solution.py:114
  17.3 34.6 %fusion.105 = f32[128,16,512]{2,0,1:T(8,128)S(1)} fusion(f32[128,16,512]{2,1,0:T(8,128)} %bitcast.269, f32[128,16,512]{2,1,0:T(8,128)} %bitcast.265, f32[512]{0:T(512)S(1)} %multiply_multiply_fusion.1, f32[128,16]{0,1:T(8,128)S(1)} %get-tuple-element.237, f32[]{:T(128)} %bitcast.16), kind=kOutput, calls=%fused_computation.193 | convolution fusion | flops 1620279296 | bytes 12593156 | tf_op jit(solution)/shard_map/ab,anl->bnl/dot_general | solution.py:13
  51.9 23.6 %fusion.103 = f32[128,16,512]{2,0,1:T(8,128)S(1)} fusion(f32[128,16,512]{2,1,0:T(8,128)S(1)} %bitcast.270, f32[128,16,512]{2,1,0:T(8,128)S(1)} %bitcast.266, f32[512]{0:T(512)S(1)} %multiply_multiply_fusion.1, f32[128,16]{0,1:T(8,128)S(1)} %get-tuple-element.237, f32[]{:T(128)} %bitcast.16), kind=kOutput, calls=%fused_computation.191 | convolution fusion | flops 1620279296 | bytes 12593156 | tf_op jit(solution)/shard_map/ab,anl->bnl/dot_general | solution.py:13
  75.6 24.7 %convolution_subtract_fusion = f32[128,16,512]{2,0,1:T(8,128)} fusion(f32[128,16,512]{2,0,1:T(8,128)S(1)} %fusion.105, f32[128,16,512]{2,1,0:T(8,128)S(1)} %bitcast.271, f32[128,16,512]{2,1,0:T(8,128)S(1)} %bitcast.267, f32[512]{0:T(512)S(1)} %multiply_multiply_fusion.1, f32[128,16]{0,1:T(8,128)S(1)} %get-tuple-element.237, f32[]{:T(128)} %bitcast.16), kind=kOutput, calls=%fused_computation.176 | convolution fusion | flops 1621327872 | bytes 16787460 | tf_op jit(solution)/shard_map/ab,anl->bnl/dot_general | solution.py:13
  100.3 25.9 %multiply_subtract_fusion.1 = (f32[128,16,512]{2,0,1:T(8,128)S(1)}, f32[128,16,512]{2,0,1:T(8,128)S(1)}) fusion(f32[128,16,512]{2,0,1:T(8,128)} %convolution_subtract_fusion, f32[128,16]{0,1:T(8,128)S(1)} %get-tuple-element.238, f32[128,16]{0,1:T(8,128)S(1)} %fusion.142, f32[128,16,512]{2,0,1:T(8,128)S(1)} %fusion.103, f32[128,16,512]{2,1,0:T(8,128)S(1)} %bitcast.272, ...), kind=kOutput, calls=%fused_computation.146 | convolution fusion | flops 1627619328 | bytes 25192452 | tf_op jit(solution)/shard_map/ab,anl->bnl/dot_general | solution.py:13
  126.3 6.6 %fusion.72 = f32[128,512,16]{1,2,0:T(8,128)S(1)} fusion(f32[128,16,512]{2,0,1:T(8,128)S(1)} %get-tuple-element.232), kind=kOutput, calls=%fused_computation.167 | convolution fusion | flops 201330176 | bytes 8388608 | tf_op jit(solution)/shard_map/nk,bnl->lkb/dot_general | solution.py:13
  132.8 6.8 %fusion.70 = f32[128,512,16]{1,2,0:T(8,128)S(1)} fusion(f32[128,16,512]{2,0,1:T(8,128)S(1)} %get-tuple-element.232), kind=kOutput, calls=%fused_computation.165 | convolution fusion | flops 201330176 | bytes 8388608 | tf_op jit(solution)/shard_map/nk,bnl->lkb/dot_general | solution.py:13
  139.7 7.1 %subtract_bitcast_fusion = f32[512,16,128]{0,1,2:T(8,128)S(1)} fusion(f32[128,512,16]{1,2,0:T(8,128)S(1)} %fusion.72, f32[128,16,512]{2,0,1:T(8,128)S(1)} %get-tuple-element.231), kind=kOutput, calls=%fused_computation.144 | convolution fusion | flops 202378752 | bytes 12582912 | tf_op jit(solution)/shard_map/nk,bnl->lkb/dot_general | solution.py:13
  149.2 7.4 %add_bitcast_fusion = f32[512,16,128]{0,1,2:T(8,128)S(1)} fusion(f32[128,512,16]{1,2,0:T(8,128)S(1)} %fusion.70, f32[128,16,512]{2,0,1:T(8,128)S(1)} %get-tuple-element.231), kind=kOutput, calls=%fused_computation.143 | convolution fusion | flops 202378752 | bytes 12582912 | tf_op jit(solution)/shard_map/nk,bnl->lkb/dot_general | solution.py:13
  160.0 16.5 %copy.84 = f32[2,512,2048]{1,0,2:T(2,128)} copy(f32[2,512,2048]{1,2,0:T(8,128)S(1)} %pad_maximum_fusion) | data formatting | bytes 16777216 | tf_op jit(solution)/shard_map/stack | solution.py:117
  176.5 5.8 %all-to-all-start.1 = ((f32[2,512,2048]{1,0,2:T(2,128)}), f32[2,512,2048]{1,0,2:T(2,128)}, u32[]{:S(2)}, u32[]{:S(2)}) async-start(f32[2,512,2048]{1,0,2:T(2,128)} %copy.84), calls=%async_computation.1 | async-start | bytes 16777216 | tf_op jit(solution)/shard_map/all_to_all | solution.py:120
  186.3 180.0 %all-to-all-done.1 = f32[2,512,2048]{1,0,2:T(2,128)} async-done(((f32[2,512,2048]{1,0,2:T(2,128)}), f32[2,512,2048]{1,0,2:T(2,128)}, u32[]{:S(2)}, u32[]{:S(2)}) %all-to-all-start.1) | async-done | bytes 8388640 | tf_op jit(solution)/shard_map/all_to_all | solution.py:120
  370.3 5.0 copy.85
  379.6 5.3 copy.88
  384.9 10.2 %fusion.64 = f32[128,16,512]{2,0,1:T(8,128)} fusion(f32[128,16,512]{2,1,0:T(8,128)} %bitcast.256), kind=kOutput, calls=%fused_computation.159 | convolution fusion | flops 1610842112 | bytes 8388608 | tf_op jit(solution)/shard_map/ab,anl->bnl/dot_general | solution.py:13
  395.1 7.1 %fusion.62 = f32[128,16,512]{2,0,1:T(8,128)} fusion(f32[128,16,512]{2,1,0:T(8,128)S(1)} %bitcast.257), kind=kOutput, calls=%fused_computation.157 | convolution fusion | flops 1610842112 | bytes 8388608 | tf_op jit(solution)/shard_map/ab,anl->bnl/dot_general | solution.py:13
  402.3 5.6 copy.86
  407.9 9.9 %fusion.82 = f32[128,16,512]{2,0,1:T(8,128)S(1)} fusion(f32[128,16,512]{2,0,1:T(8,128)} %fusion.64, f32[128,16,512]{2,1,0:T(8,128)} %bitcast.254), kind=kOutput, calls=%fused_computation.173 | convolution fusion | flops 1611890688 | bytes 12582912 | tf_op jit(solution)/shard_map/ab,anl->bnl/dot_general | solution.py:13
  417.8 7.5 %multiply_subtract_fusion = (f32[128,16,512]{2,0,1:T(8,128)S(1)}, f32[128,16,512]{2,0,1:T(8,128)S(1)}) fusion(f32[128,16,512]{2,0,1:T(8,128)S(1)} %fusion.82, f32[128,16]{0,1:T(8,128)S(1)} %get-tuple-element.238, f32[128,16]{0,1:T(8,128)S(1)} %fusion.142, f32[128,16,512]{2,0,1:T(8,128)S(1)} %copy-done.2, f32[128,16,512]{2,1,0:T(8,128)S(1)} %bitcast.255), kind=kOutput, calls=%fused_computation.142 | convolution fusion | flops 1618182144 | bytes 20987904 | tf_op jit(solution)/shard_map/ab,anl->bnl/dot_general | solution.py:13
  425.3 5.6 fusion.56
  430.9 5.8 %fusion.54 = f32[16,128,512]{2,0,1:T(8,128)S(1)} fusion(f32[128,16,512]{2,0,1:T(8,128)S(1)} %get-tuple-element.230), kind=kOutput, calls=%fused_computation.149 | convolution fusion | flops 201330176 | bytes 8388608 | tf_op jit(solution)/shard_map/nk,bnl->kbl/dot_general | solution.py:13
  436.7 6.1 %subtract_multiply_fusion = f32[16,128,512]{2,0,1:T(8,128)S(1)} fusion(f32[16,128,512]{2,0,1:T(8,128)S(1)} %fusion.56, f32[128,16,512]{2,0,1:T(8,128)S(1)} %get-tuple-element.229), kind=kOutput, calls=%fused_computation.140 | convolution fusion | flops 203427328 | bytes 12582912 | tf_op jit(solution)/shard_map/nk,bnl->kbl/dot_general | solution.py:13
  445.2 6.0 %add_multiply_fusion = f32[16,128,512]{2,0,1:T(8,128)S(1)} fusion(f32[16,128,512]{2,0,1:T(8,128)S(1)} %fusion.54, f32[128,16,512]{2,0,1:T(8,128)S(1)} %get-tuple-element.229), kind=kOutput, calls=%fused_computation.139 | convolution fusion | flops 203427328 | bytes 12582912 | tf_op jit(solution)/shard_map/nk,bnl->kbl/dot_general | solution.py:13
  457.9 107.1 %while.16 = (s32[]{:T(128)}, f32[2,8,2,512]{3,2,1,0:T(2,128)}, s32[2,8]{1,0:T(2,128)S(1)}, s32[]{:T(128)}, f32[2,2048,512]{2,1,0:T(8,128)}, /*index=5*/s32[2,8,2...) while((s32[]{:T(128)}, f32[2,8,2,512]{3,2,1,0:T(2,128)}, ...), condition=%wide.region_6.7_spmd, body=%wide.region_4.6_spmd.sunk | while | flops 1649795328 | bytes 12208282 | solution.py:95
  458.4 8.9 %select_add_fusion.2 = f32[8,512,128]{2,1,0:T(8,128)S(1)} fusion(f32[8,512]{1,0:T(8,128)S(1)} %bitcast.273, s32[8,512]{1,0:T(8,128)S(1)} %get-tuple-element.360, f32[8,512]{1,0:T(8,128)S(1)} %bitcast.274, s32[8,512]{1,0:T(8,128)S(1)} %get-tuple-element.362, f32[8,512]{1,0:T(8,128)S(1)} %bitcast.275, s32[8,512]{1,0:T(8,128)S(1)} %get-tuple-element.364, ...), kind=kLoop, calls=%fused_computation.8.clone.1 | loop fusion | flops 12058624 | bytes 2359296 | tf_op jit(solution)/shard_map/while/body/eval_jaxpr/add | solution.py:67
  469.7 23.6 %while.17 = (s32[]{:T(128)}, f32[2,2048,512]{2,1,0:T(8,128)}, s32[8,3]{0,1:T(4,128)S(1)}, f32[8,2,128,128]{3,2,1,0:T(8,128)S(1)}, s32[]{:T(128)}) while((s32[]{:T(128)}, f32[2,2048,512]{2,1,0:T(8,128)}, s32[8,3]{0,1:T(4,128)S(1)}, f32[8,2,128,128]{3,2,1,0:T(8,128)S(1)}, s32[]{:T(128)}) %tuple.108), condition=%wide.while_cond, body=%wide.while_body.sunk | while | flops 2 | bytes 262261 | solution.py:149
  493.3 17.5 %fusion.249 = f32[8,2,512]{2,1,0:T(2,128)S(1)} fusion(f32[8,2,128,128]{3,2,1,0:T(8,128)S(1)} %get-tuple-element.354, f32[8,512,128]{1,2,0:T(8,128)} %copy.239, f32[8,512]{1,0:T(8,128)S(1)} %bitcast.282, s32[8,512]{1,0:T(8,128)S(1)} %get-tuple-element.377, f32[8,512]{1,0:T(8,128)S(1)} %bitcast.283, s32[8,512]{1,0:T(8,128)S(1)} %get-tuple-element.379, ...), kind=kOutput, calls=%fused_computation.6.clone.2 | convolution fusion | flops 1624760320 | bytes 3440640 | tf_op jit(solution)/shard_map/while/body/eval_jaxpr/gsu,gcuv->gcsv/dot_general | solution.py:13
  511.9 8.9 %select_add_fusion.2 = f32[8,512,128]{2,1,0:T(8,128)S(1)} fusion(f32[8,512]{1,0:T(8,128)S(1)} %bitcast.273, s32[8,512]{1,0:T(8,128)S(1)} %get-tuple-element.360, f32[8,512]{1,0:T(8,128)S(1)} %bitcast.274, s32[8,512]{1,0:T(8,128)S(1)} %get-tuple-element.362, f32[8,512]{1,0:T(8,128)S(1)} %bitcast.275, s32[8,512]{1,0:T(8,128)S(1)} %get-tuple-element.364, ...), kind=kLoop, calls=%fused_computation.8.clone.1 | loop fusion | flops 12058624 | bytes 2359296 | tf_op jit(solution)/shard_map/while/body/eval_jaxpr/add | solution.py:67
  523.3 23.7 %while.17 = (s32[]{:T(128)}, f32[2,2048,512]{2,1,0:T(8,128)}, s32[8,3]{0,1:T(4,128)S(1)}, f32[8,2,128,128]{3,2,1,0:T(8,128)S(1)}, s32[]{:T(128)}) while((s32[]{:T(128)}, f32[2,2048,512]{2,1,0:T(8,128)}, s32[8,3]{0,1:T(4,128)S(1)}, f32[8,2,128,128]{3,2,1,0:T(8,128)S(1)}, s32[]{:T(128)}) %tuple.108), condition=%wide.while_cond, body=%wide.while_body.sunk | while | flops 2 | bytes 262261 | solution.py:149
  546.9 17.5 %fusion.249 = f32[8,2,512]{2,1,0:T(2,128)S(1)} fusion(f32[8,2,128,128]{3,2,1,0:T(8,128)S(1)} %get-tuple-element.354, f32[8,512,128]{1,2,0:T(8,128)} %copy.239, f32[8,512]{1,0:T(8,128)S(1)} %bitcast.282, s32[8,512]{1,0:T(8,128)S(1)} %get-tuple-element.377, f32[8,512]{1,0:T(8,128)S(1)} %bitcast.283, s32[8,512]{1,0:T(8,128)S(1)} %get-tuple-element.379, ...), kind=kOutput, calls=%fused_computation.6.clone.2 | convolution fusion | flops 1624760320 | bytes 3440640 | tf_op jit(solution)/shard_map/while/body/eval_jaxpr/gsu,gcuv->gcsv/dot_general | solution.py:13
  569.4 5.0 all-to-all-done.3
  (157 shorter events, 90.2 us)
Async XLA Ops:
  3.7 172.8 %all-to-all-start = ((s32[8,1,2]{2,1,0:T(1,128)}), s32[8,1,2]{2,1,0:T(1,128)S(1)}, u32[]{:S(2)}, u32[]{:S(2)}) async-start(s32[8,1,2]{2,1,0:T(1,128)} %bitcast.12), calls=%async_computation | async-start | bytes 8192 | tf_op jit(solution)/shard_map/all_to_all | solution.py:161
  17.3 34.6 %copy-start.3 = (f32[1,2048,512]{2,1,0:T(8,128)S(1)}, f32[1,2048,512]{2,1,0:T(8,128)}, u32[]{:S(2)}) copy-start(f32[1,2048,512]{2,1,0:T(8,128)} %get-tuple-element.235) | copy-start | bytes 12582916
  17.3 34.6 %copy-start.4 = (f32[1,2048,512]{2,1,0:T(8,128)S(1)}, f32[1,2048,512]{2,1,0:T(8,128)}, u32[]{:S(2)}) copy-start(f32[1,2048,512]{2,1,0:T(8,128)} %get-tuple-element.236) | copy-start | bytes 12582916
  176.5 6.4 %copy-start.6 = (s32[16,2,512]{2,1,0:T(2,128)S(1)}, s32[16,2,512]{2,1,0:T(2,128)}, u32[]{:S(2)}) copy-start(s32[16,2,512]{2,1,0:T(2,128)} %param.14) | copy-start | bytes 196612
  176.5 189.8 %all-to-all-start.1 = ((f32[2,512,2048]{1,0,2:T(2,128)}), f32[2,512,2048]{1,0,2:T(2,128)}, u32[]{:S(2)}, u32[]{:S(2)}) async-start(f32[2,512,2048]{1,0,2:T(2,128)} %copy.84), calls=%async_computation.1 | async-start | bytes 16777216 | tf_op jit(solution)/shard_map/all_to_all | solution.py:120
  366.3 91.6 %all-to-all-start.2 = ((s32[8,2,2,512]{3,2,1,0:T(2,128)}), s32[8,2,2,512]{3,2,1,0:T(2,128)S(1)}, u32[]{:S(2)}, u32[]{:S(2)}) async-start(s32[8,2,2,512]{3,2,1,0:T(2,128)} %bitcast.31), calls=%async_computation.2 | async-start | bytes 131072 | tf_op jit(solution)/shard_map/all_to_all | solution.py:162
  384.9 10.2 %copy-start.1 = (f32[1,4,512,512]{3,2,1,0:T(8,128)S(1)}, f32[1,4,512,512]{3,2,1,0:T(8,128)}, u32[]{:S(2)}) copy-start(f32[1,4,512,512]{3,2,1,0:T(8,128)} %copy.88) | copy-start | bytes 12582916
  407.9 9.9 %copy-start = (f32[1,4,512,512]{3,2,1,0:T(8,128)S(1)}, f32[1,4,512,512]{3,2,1,0:T(8,128)}, u32[]{:S(2)}) copy-start(f32[1,4,512,512]{3,2,1,0:T(8,128)} %copy.86) | copy-start | bytes 12582916
  407.9 9.9 %copy-start.2 = (f32[128,16,512]{2,0,1:T(8,128)S(1)}, f32[128,16,512]{2,0,1:T(8,128)}, u32[]{:S(2)}) copy-start(f32[128,16,512]{2,0,1:T(8,128)} %fusion.62) | copy-start | bytes 12582916
  453.7 4.2 copy-start.5
  457.9 117.1 %copy-start.7 = (f32[16,2,512]{2,1,0:T(2,128)S(1)}, f32[16,2,512]{2,1,0:T(2,128)}, u32[]{:S(2)}) copy-start(f32[16,2,512]{2,1,0:T(2,128)} %param.15) | copy-start | bytes 196612
  565.0 9.4 %all-to-all-start.3 = ((f32[8,2,2,512]{3,2,1,0:T(2,128)}), f32[8,2,2,512]{3,2,1,0:T(2,128)S(1)}, u32[]{:S(2)}, u32[]{:S(2)}) async-start(f32[8,2,2,512]{3,2,1,0:T(2,128)} %bitcast.33), calls=%async_computation.3 | async-start | bytes 131072 | tf_op jit(solution)/shard_map/all_to_all | solution.py:172
where the time goes:
time: 587 us; the launch traced here: 576 us
  matrix products  231 us (39%)
  waiting for transfers between devices  185 us (32%)
  local copies, waits for them, and re-layouts  112 us (19%)
  other arithmetic  27.1 us (5%)
  starting transfers between devices  19.3 us (3%)
    dot_general x22, matrix products, product(): return jnp.einsum(pattern, operand_a, operand_b, precision=PRECISE)  231 us
    all_to_all x1, waiting for transfers between devices, shards(): lax.all_to_all(stacked, 'wa', split_axis=2, concat_axis=1, tiled=True)  180 us
    gather x48, local copies, waits for them, and re-layouts  47 us
    add x2, other arithmetic, kernel_rows(): weights + jnp.where(tile_cells == cell_index[..., None] + tap_step, kerne...  17.9 us
    another operation x1, local copies, waits for them, and re-layouts, shards(): jnp.stack([half_done[0].reshape(column_count, extent), half_done[1].resha...  16.5 us
    slice x3, local copies, waits for them, and re-layouts, shards(): finished = transform((exchanged[0], exchanged[1]), 'kbl')  15.2 us
  transfers between devices with their start and end apart: 4, of which 2 were waited for; matrix products, arithmetic and copies ran while one was open for 45% of the time, Pallas kernels for 0%

commit v1 on v0

--- a/solution.py
+++ b/solution.py
@@ -117,7 +117,10 @@
     stacked = jnp.stack(
         [half_done[0].reshape(column_count, extent), half_done[1].reshape(column_count, extent)]
     )
-    exchanged = lax.all_to_all(stacked, "wa", split_axis=2, concat_axis=1, tiled=True)
+    count_2 = lax.axis_size("wa")
+    blocks = jnp.stack(jnp.split(stacked, count_2, axis=2), axis=0)
+    blocks = lax.all_to_all(blocks, "wa", split_axis=0, concat_axis=0)
+    exchanged = jnp.concatenate(blocks, axis=1)
     finished = transform((exchanged[0], exchanged[1]), "kbl")
     norm_factor = 1.0 / extent
     uv_grid = jnp.stack(

time: 587 us -> 566 us (0.964)
  local copies, waits for them, and re-layouts: 112 us -> 95.1 us
  matrix products: 231 us -> 222 us
    another operation x3 -> x2, local copies, waits for them, and re-layouts: 16.5 us -> 0.01 us  [the longest x1 16.5 us: shards(): jnp.stack([half_done[0].reshape(column_count, extent), half_done[1].resha...]
    dot_general x22, matrix products: 231 us -> 222 us  [product(): return jnp.einsum(pattern, operand_a, operand_b, precision=PRECISE)]
  transfers between devices with their start and end apart: 4 -> 4, of which waited for: 2 -> 2; matrix products, arithmetic and copies ran while one was open for 45% -> 42% of each run, Pallas kernels for 0% -> 0%
where the time goes in v1:
time: 566 us; the launch traced here: 555 us
  matrix products  222 us (39%)
  waiting for transfers between devices  185 us (33%)
  local copies, waits for them, and re-layouts  95.1 us (17%)
  other arithmetic  31 us (5%)
  starting transfers between devices  19.3 us (3%)
    dot_general x22, matrix products, product(): return jnp.einsum(pattern, operand_a, operand_b, precision=PRECISE)  222 us
    all_to_all x1, waiting for transfers between devices, shards(): blocks = lax.all_to_all(blocks, 'wa', split_axis=0, concat_axis=0)  180 us
    gather x48, local copies, waits for them, and re-layouts  48.4 us
    slice x3, local copies, waits for them, and re-layouts, shards(): finished = transform((exchanged[0], exchanged[1]), 'kbl')  18.4 us
    add x2, other arithmetic, kernel_rows(): weights + jnp.where(tile_cells == cell_index[..., None] + tap_step, kerne...  17.9 us
  transfers between devices with their start and end apart: 4, of which 2 were waited for; matrix products, arithmetic and copies ran while one was open for 42% of the time, Pallas kernels for 0%

profile of v1, /device:TPU:0, one launch (start us, length us, event | category | flops | bytes accessed | tf_op | source)
XLA Modules:
  0.0 554.7 jit_solution(4152562422710093425)
XLA Ops:
  3.7 5.2 all-to-all-start
  9.0 7.7 %fusion.233 = (f32[1,2048,512]{2,1,0:T(8,128)}, f32[1,2048,512]{2,1,0:T(8,128)}) fusion(f32[2,2048,512]{2,1,0:T(8,128)} %param.9), kind=kLoop, calls=%fused_computation.323 | loop fusion | bytes 16777216 | tf_op jit(solution)/shard_map/slice | solution.py:114
  17.3 26.0 %fusion.112 = f32[128,16,512]{2,0,1:T(8,128)S(1)} fusion(f32[128,16,512]{2,1,0:T(8,128)} %bitcast.274, f32[128,16,512]{2,1,0:T(8,128)} %bitcast.270, f32[512]{0:T(512)S(1)} %multiply_multiply_fusion.1, f32[128,16]{0,1:T(8,128)S(1)} %get-tuple-element.234, f32[]{:T(128)} %bitcast.16), kind=kOutput, calls=%fused_computation.207 | convolution fusion | flops 1620279296 | bytes 12593156 | tf_op jit(solution)/shard_map/ab,anl->bnl/dot_general | solution.py:13
  43.4 23.4 %fusion.110 = f32[128,16,512]{2,0,1:T(8,128)S(1)} fusion(f32[128,16,512]{2,1,0:T(8,128)S(1)} %bitcast.275, f32[128,16,512]{2,1,0:T(8,128)S(1)} %bitcast.271, f32[512]{0:T(512)S(1)} %multiply_multiply_fusion.1, f32[128,16]{0,1:T(8,128)S(1)} %get-tuple-element.234, f32[]{:T(128)} %bitcast.16), kind=kOutput, calls=%fused_computation.205 | convolution fusion | flops 1620279296 | bytes 12593156 | tf_op jit(solution)/shard_map/ab,anl->bnl/dot_general | solution.py:13
  66.9 24.7 %convolution_subtract_fusion = f32[128,16,512]{2,0,1:T(8,128)} fusion(f32[128,16,512]{2,0,1:T(8,128)S(1)} %fusion.112, f32[128,16,512]{2,1,0:T(8,128)S(1)} %bitcast.276, f32[128,16,512]{2,1,0:T(8,128)S(1)} %bitcast.272, f32[512]{0:T(512)S(1)} %multiply_multiply_fusion.1, f32[128,16]{0,1:T(8,128)S(1)} %get-tuple-element.234, f32[]{:T(128)} %bitcast.16), kind=kOutput, calls=%fused_computation.182 | convolution fusion | flops 1621327872 | bytes 16787460 | tf_op jit(solution)/shard_map/ab,anl->bnl/dot_general | solution.py:13
  91.6 25.9 %multiply_subtract_fusion.1 = (f32[128,16,512]{2,0,1:T(8,128)S(1)}, f32[128,16,512]{2,0,1:T(8,128)S(1)}) fusion(f32[128,16,512]{2,0,1:T(8,128)} %convolution_subtract_fusion, f32[128,16]{0,1:T(8,128)S(1)} %get-tuple-element.235, f32[128,16]{0,1:T(8,128)S(1)} %fusion.149, f32[128,16,512]{2,0,1:T(8,128)S(1)} %fusion.110, f32[128,16,512]{2,1,0:T(8,128)S(1)} %bitcast.277, ...), kind=kOutput, calls=%fused_computation.152 | convolution fusion | flops 1627619328 | bytes 25192452 | tf_op jit(solution)/shard_map/ab,anl->bnl/dot_general | solution.py:13
  117.5 6.6 %fusion.70 = f32[128,512,16]{1,2,0:T(8,128)S(1)} fusion(f32[128,16,512]{2,0,1:T(8,128)S(1)} %get-tuple-element.225), kind=kOutput, calls=%fused_computation.171 | convolution fusion | flops 201330176 | bytes 8388608 | tf_op jit(solution)/shard_map/nk,bnl->lkb/dot_general | solution.py:13
  124.1 6.8 %fusion.72 = f32[128,512,16]{1,2,0:T(8,128)S(1)} fusion(f32[128,16,512]{2,0,1:T(8,128)S(1)} %get-tuple-element.225), kind=kOutput, calls=%fused_computation.173 | convolution fusion | flops 201330176 | bytes 8388608 | tf_op jit(solution)/shard_map/nk,bnl->lkb/dot_general | solution.py:13
  130.9 7.0 %add_bitcast_fusion = f32[512,16,128]{0,1,2:T(8,128)S(1)} fusion(f32[128,512,16]{1,2,0:T(8,128)S(1)} %fusion.70, f32[128,16,512]{2,0,1:T(8,128)S(1)} %get-tuple-element.224), kind=kOutput, calls=%fused_computation.149 | convolution fusion | flops 202378752 | bytes 12582912 | tf_op jit(solution)/shard_map/nk,bnl->lkb/dot_general | solution.py:13
  140.4 7.5 %subtract_bitcast_fusion = f32[512,16,128]{0,1,2:T(8,128)S(1)} fusion(f32[128,512,16]{1,2,0:T(8,128)S(1)} %fusion.72, f32[128,16,512]{2,0,1:T(8,128)S(1)} %get-tuple-element.224), kind=kOutput, calls=%fused_computation.150 | convolution fusion | flops 202378752 | bytes 12582912 | tf_op jit(solution)/shard_map/nk,bnl->lkb/dot_general | solution.py:13
  155.3 5.8 %all-to-all-start.1 = ((f32[4,2,512,512]{2,3,1,0:T(8,128)}), f32[4,2,512,512]{2,3,1,0:T(8,128)}, u32[]{:S(2)}, u32[]{:S(2)}) async-start(f32[4,2,512,512]{2,3,1,0:T(8,128)} %pad_maximum_fusion), calls=%async_computation.1 | async-start | bytes 16777216 | tf_op jit(solution)/shard_map/all_to_all | solution.py:122
  165.1 180.1 %all-to-all-done.1 = f32[4,2,512,512]{2,3,1,0:T(8,128)} async-done(((f32[4,2,512,512]{2,3,1,0:T(8,128)}), f32[4,2,512,512]{2,3,1,0:T(8,128)}, u32[]{:S(2)}, u32[]{:S(2)}) %all-to-all-start.1) | async-done | bytes 8388640 | tf_op jit(solution)/shard_map/all_to_all | solution.py:122
  349.1 7.7 %fusion.232 = (f32[1,4,512,512]{2,3,0,1:T(8,128)}, f32[1,4,512,512]{2,3,0,1:T(8,128)}) fusion(f32[2,4,512,512]{2,3,0,1:T(8,128)} %bitcast.28), kind=kLoop, calls=%fused_computation.322 | loop fusion | bytes 16777216 | tf_op jit(solution)/shard_map/slice | solution.py:124
  356.8 5.3 copy.62
  362.1 10.2 %fusion.64 = f32[128,16,512]{2,0,1:T(8,128)} fusion(f32[128,16,512]{2,1,0:T(8,128)} %bitcast.262), kind=kOutput, calls=%fused_computation.165 | convolution fusion | flops 1610842112 | bytes 8388608 | tf_op jit(solution)/shard_map/ab,anl->bnl/dot_general | solution.py:13
  372.3 7.2 %fusion.62 = f32[128,16,512]{2,0,1:T(8,128)} fusion(f32[128,16,512]{2,1,0:T(8,128)S(1)} %bitcast.263), kind=kOutput, calls=%fused_computation.163 | convolution fusion | flops 1610842112 | bytes 8388608 | tf_op jit(solution)/shard_map/ab,anl->bnl/dot_general | solution.py:13
  379.5 5.4 copy.60
  385.0 9.9 %fusion.82 = f32[128,16,512]{2,0,1:T(8,128)S(1)} fusion(f32[128,16,512]{2,0,1:T(8,128)} %fusion.64, f32[128,16,512]{2,1,0:T(8,128)} %bitcast.260), kind=kOutput, calls=%fused_computation.179 | convolution fusion | flops 1611890688 | bytes 12582912 | tf_op jit(solution)/shard_map/ab,anl->bnl/dot_general | solution.py:13
  394.9 7.7 %multiply_subtract_fusion = (f32[128,16,512]{2,0,1:T(8,128)S(1)}, f32[128,16,512]{2,0,1:T(8,128)S(1)}) fusion(f32[128,16,512]{2,0,1:T(8,128)S(1)} %fusion.82, f32[128,16]{0,1:T(8,128)S(1)} %get-tuple-element.235, f32[128,16]{0,1:T(8,128)S(1)} %fusion.149, f32[128,16,512]{2,0,1:T(8,128)S(1)} %copy-done.2, f32[128,16,512]{2,1,0:T(8,128)S(1)} %bitcast.261), kind=kOutput, calls=%fused_computation.148 | convolution fusion | flops 1618182144 | bytes 20987904 | tf_op jit(solution)/shard_map/ab,anl->bnl/dot_general | solution.py:13
  402.6 5.6 %fusion.56 = f32[16,128,512]{2,0,1:T(8,128)S(1)} fusion(f32[128,16,512]{2,0,1:T(8,128)S(1)} %get-tuple-element.223), kind=kOutput, calls=%fused_computation.157 | convolution fusion | flops 201330176 | bytes 8388608 | tf_op jit(solution)/shard_map/nk,bnl->kbl/dot_general | solution.py:13
  408.2 5.8 %fusion.54 = f32[16,128,512]{2,0,1:T(8,128)S(1)} fusion(f32[128,16,512]{2,0,1:T(8,128)S(1)} %get-tuple-element.223), kind=kOutput, calls=%fused_computation.155 | convolution fusion | flops 201330176 | bytes 8388608 | tf_op jit(solution)/shard_map/nk,bnl->kbl/dot_general | solution.py:13
  414.0 6.1 %subtract_multiply_fusion = f32[16,128,512]{2,0,1:T(8,128)S(1)} fusion(f32[16,128,512]{2,0,1:T(8,128)S(1)} %fusion.56, f32[128,16,512]{2,0,1:T(8,128)S(1)} %get-tuple-element.222), kind=kOutput, calls=%fused_computation.146 | convolution fusion | flops 203427328 | bytes 12582912 | tf_op jit(solution)/shard_map/nk,bnl->kbl/dot_general | solution.py:13
  422.5 6.0 %add_multiply_fusion = f32[16,128,512]{2,0,1:T(8,128)S(1)} fusion(f32[16,128,512]{2,0,1:T(8,128)S(1)} %fusion.54, f32[128,16,512]{2,0,1:T(8,128)S(1)} %get-tuple-element.222), kind=kOutput, calls=%fused_computation.145 | convolution fusion | flops 203427328 | bytes 12582912 | tf_op jit(solution)/shard_map/nk,bnl->kbl/dot_general | solution.py:13
  435.1 108.6 %while.16 = (s32[]{:T(128)}, f32[2,8,2,512]{3,2,1,0:T(2,128)}, s32[2,8]{1,0:T(2,128)S(1)}, s32[]{:T(128)}, f32[2,2048,512]{2,1,0:T(8,128)}, /*index=5*/s32[2,8,2...) while((s32[]{:T(128)}, f32[2,8,2,512]{3,2,1,0:T(2,128)}, ...), condition=%wide.region_6.7_spmd, body=%wide.region_4.6_spmd.sunk | while | flops 1649795328 | bytes 12208282 | solution.py:95
  435.6 8.9 %select_add_fusion.2 = f32[8,512,128]{2,1,0:T(8,128)S(1)} fusion(f32[8,512]{1,0:T(8,128)S(1)} %bitcast.278, s32[8,512]{1,0:T(8,128)S(1)} %get-tuple-element.357, f32[8,512]{1,0:T(8,128)S(1)} %bitcast.279, s32[8,512]{1,0:T(8,128)S(1)} %get-tuple-element.359, f32[8,512]{1,0:T(8,128)S(1)} %bitcast.280, s32[8,512]{1,0:T(8,128)S(1)} %get-tuple-element.361, ...), kind=kLoop, calls=%fused_computation.8.clone.1 | loop fusion | flops 12058624 | bytes 2359296 | tf_op jit(solution)/shard_map/while/body/eval_jaxpr/add | solution.py:67
  446.9 24.3 %while.17 = (s32[]{:T(128)}, f32[2,2048,512]{2,1,0:T(8,128)}, s32[8,3]{0,1:T(4,128)S(1)}, f32[8,2,128,128]{3,2,1,0:T(8,128)S(1)}, s32[]{:T(128)}) while((s32[]{:T(128)}, f32[2,2048,512]{2,1,0:T(8,128)}, s32[8,3]{0,1:T(4,128)S(1)}, f32[8,2,128,128]{3,2,1,0:T(8,128)S(1)}, s32[]{:T(128)}) %tuple.110), condition=%wide.while_cond, body=%wide.while_body.sunk | while | flops 2 | bytes 262261 | solution.py:152
  471.3 17.5 %fusion.256 = f32[8,2,512]{2,1,0:T(2,128)S(1)} fusion(f32[8,2,128,128]{3,2,1,0:T(8,128)S(1)} %get-tuple-element.351, f32[8,512,128]{1,2,0:T(8,128)} %copy.213, f32[8,512]{1,0:T(8,128)S(1)} %bitcast.287, s32[8,512]{1,0:T(8,128)S(1)} %get-tuple-element.374, f32[8,512]{1,0:T(8,128)S(1)} %bitcast.288, s32[8,512]{1,0:T(8,128)S(1)} %get-tuple-element.376, ...), kind=kOutput, calls=%fused_computation.6.clone.2 | convolution fusion | flops 1624760320 | bytes 3440640 | tf_op jit(solution)/shard_map/while/body/eval_jaxpr/gsu,gcuv->gcsv/dot_general | solution.py:13
  489.9 8.9 %select_add_fusion.2 = f32[8,512,128]{2,1,0:T(8,128)S(1)} fusion(f32[8,512]{1,0:T(8,128)S(1)} %bitcast.278, s32[8,512]{1,0:T(8,128)S(1)} %get-tuple-element.357, f32[8,512]{1,0:T(8,128)S(1)} %bitcast.279, s32[8,512]{1,0:T(8,128)S(1)} %get-tuple-element.359, f32[8,512]{1,0:T(8,128)S(1)} %bitcast.280, s32[8,512]{1,0:T(8,128)S(1)} %get-tuple-element.361, ...), kind=kLoop, calls=%fused_computation.8.clone.1 | loop fusion | flops 12058624 | bytes 2359296 | tf_op jit(solution)/shard_map/while/body/eval_jaxpr/add | solution.py:67
  501.2 24.4 %while.17 = (s32[]{:T(128)}, f32[2,2048,512]{2,1,0:T(8,128)}, s32[8,3]{0,1:T(4,128)S(1)}, f32[8,2,128,128]{3,2,1,0:T(8,128)S(1)}, s32[]{:T(128)}) while((s32[]{:T(128)}, f32[2,2048,512]{2,1,0:T(8,128)}, s32[8,3]{0,1:T(4,128)S(1)}, f32[8,2,128,128]{3,2,1,0:T(8,128)S(1)}, s32[]{:T(128)}) %tuple.110), condition=%wide.while_cond, body=%wide.while_body.sunk | while | flops 2 | bytes 262261 | solution.py:152
  525.6 17.5 %fusion.256 = f32[8,2,512]{2,1,0:T(2,128)S(1)} fusion(f32[8,2,128,128]{3,2,1,0:T(8,128)S(1)} %get-tuple-element.351, f32[8,512,128]{1,2,0:T(8,128)} %copy.213, f32[8,512]{1,0:T(8,128)S(1)} %bitcast.287, s32[8,512]{1,0:T(8,128)S(1)} %get-tuple-element.374, f32[8,512]{1,0:T(8,128)S(1)} %bitcast.288, s32[8,512]{1,0:T(8,128)S(1)} %get-tuple-element.376, ...), kind=kOutput, calls=%fused_computation.6.clone.2 | convolution fusion | flops 1624760320 | bytes 3440640 | tf_op jit(solution)/shard_map/while/body/eval_jaxpr/gsu,gcuv->gcsv/dot_general | solution.py:13
  543.7 4.3 all-to-all-start.3
  548.0 5.0 all-to-all-done.3
  (156 shorter events, 87.0 us)
Async XLA Ops:
  3.7 151.6 %all-to-all-start = ((s32[8,1,2]{2,1,0:T(1,128)}), s32[8,1,2]{2,1,0:T(1,128)S(1)}, u32[]{:S(2)}, u32[]{:S(2)}) async-start(s32[8,1,2]{2,1,0:T(1,128)} %bitcast.12), calls=%async_computation | async-start | bytes 8192 | tf_op jit(solution)/shard_map/all_to_all | solution.py:164
  17.3 26.1 %copy-start.3 = (f32[1,2048,512]{2,1,0:T(8,128)S(1)}, f32[1,2048,512]{2,1,0:T(8,128)}, u32[]{:S(2)}) copy-start(f32[1,2048,512]{2,1,0:T(8,128)} %get-tuple-element.232) | copy-start | bytes 12582916
  17.3 26.1 %copy-start.4 = (f32[1,2048,512]{2,1,0:T(8,128)S(1)}, f32[1,2048,512]{2,1,0:T(8,128)}, u32[]{:S(2)}) copy-start(f32[1,2048,512]{2,1,0:T(8,128)} %get-tuple-element.233) | copy-start | bytes 12582916
  155.3 6.4 %copy-start.6 = (s32[16,2,512]{2,1,0:T(2,128)S(1)}, s32[16,2,512]{2,1,0:T(2,128)}, u32[]{:S(2)}) copy-start(s32[16,2,512]{2,1,0:T(2,128)} %param.14) | copy-start | bytes 196612
  155.3 189.8 %all-to-all-start.1 = ((f32[4,2,512,512]{2,3,1,0:T(8,128)}), f32[4,2,512,512]{2,3,1,0:T(8,128)}, u32[]{:S(2)}, u32[]{:S(2)}) async-start(f32[4,2,512,512]{2,3,1,0:T(8,128)} %pad_maximum_fusion), calls=%async_computation.1 | async-start | bytes 16777216 | tf_op jit(solution)/shard_map/all_to_all | solution.py:122
  345.1 90.0 %all-to-all-start.2 = ((s32[8,2,2,512]{3,2,1,0:T(2,128)}), s32[8,2,2,512]{3,2,1,0:T(2,128)S(1)}, u32[]{:S(2)}, u32[]{:S(2)}) async-start(s32[8,2,2,512]{3,2,1,0:T(2,128)} %bitcast.33), calls=%async_computation.2 | async-start | bytes 131072 | tf_op jit(solution)/shard_map/all_to_all | solution.py:165
  362.1 10.2 %copy-start.1 = (f32[1,4,512,512]{3,2,1,0:T(8,128)S(1)}, f32[1,4,512,512]{3,2,1,0:T(8,128)}, u32[]{:S(2)}) copy-start(f32[1,4,512,512]{3,2,1,0:T(8,128)} %copy.62) | copy-start | bytes 12582916
  385.0 9.9 %copy-start = (f32[1,4,512,512]{3,2,1,0:T(8,128)S(1)}, f32[1,4,512,512]{3,2,1,0:T(8,128)}, u32[]{:S(2)}) copy-start(f32[1,4,512,512]{3,2,1,0:T(8,128)} %copy.60) | copy-start | bytes 12582916
  385.0 9.9 %copy-start.2 = (f32[128,16,512]{2,0,1:T(8,128)S(1)}, f32[128,16,512]{2,0,1:T(8,128)}, u32[]{:S(2)}) copy-start(f32[128,16,512]{2,0,1:T(8,128)} %fusion.62) | copy-start | bytes 12582916
  430.9 4.2 copy-start.5
  435.1 118.6 %copy-start.7 = (f32[16,2,512]{2,1,0:T(2,128)S(1)}, f32[16,2,512]{2,1,0:T(2,128)}, u32[]{:S(2)}) copy-start(f32[16,2,512]{2,1,0:T(2,128)} %param.15) | copy-start | bytes 196612
  543.7 9.3 %all-to-all-start.3 = ((f32[8,2,2,512]{3,2,1,0:T(2,128)}), f32[8,2,2,512]{3,2,1,0:T(2,128)S(1)}, u32[]{:S(2)}, u32[]{:S(2)}) async-start(f32[8,2,2,512]{3,2,1,0:T(2,128)} %bitcast.35), calls=%async_computation.3 | async-start | bytes 131072 | tf_op jit(solution)/shard_map/all_to_all | solution.py:175
